TPU v7x, 1024 devices: a whole 8x8x8 slice. The times are simulated.
1024 devices in a mesh: pipe: 4 (over y_hi, core), expert: 64 (over z, x), tensor: 4 (over y_lo).
Axes of the slice: x: 8, y: 8 (y_hi: 2, y_lo: 4; y = y_hi * 4 + y_lo), z: 8, core: 2. Of those that a mesh axis runs over, the one named last changes fastest.
Arguments:
- stream: bfloat16 [2, 4, 1024, 7168], P(None, 'pipe', 'expert', 'tensor'), may hold values from -6 to 6
- expert_ids: int32 [2, 4, 1024, 8], P(None, 'pipe', 'expert'), may hold values from 0 to 63, all different within a row; in each aligned block of 16 rows (0 to 15, 16 to 31, ..., all dimensions but the last counted through in order) at most 3 rows name the same one
- norm_gain: float32 [4, 7168], P('pipe', 'tensor'), may hold values from 0.1 to 1.9
- router: float32 [4, 7168, 64], P('pipe', 'tensor'), may hold values from -0.0625 to 0.0625
- w_up: bfloat16 [64, 7168, 1024], P('expert', 'tensor'), may hold values from -0.0625 to 0.0625
- w_down: bfloat16 [64, 1024, 7168], P('expert', None, 'tensor'), may hold values from -0.1875 to 0.1875
Outputs:
- result: bfloat16 [2, 4, 1024, 7168], P(None, 'pipe', 'expert', 'tensor')
Inputs may be any that keep to these rules, and one draw needn't show every extreme that they name: `expert_ids`: each token names 8 different experts. Among the 16 tokens of one direction held by one index of the expert axis at one section, at most 3 name any one expert, and in every draw some expert is named by exactly 3 of them.
All inputs are finite; a program needn't handle non-finite values.
Results may differ from a plain program's by a relative error of at most 0.0065.
Values may be sent and summed in bfloat16 or wider, within the bound.
A program may use at most 32 MiB of HBM per device.

v0:
```python
import jax
import jax.numpy as jnp
from jax import lax
from jax.sharding import PartitionSpec as P

norm_eps = 1e-06
route_scale = 2.5


def shifted(x, axis, by):
    size = lax.axis_size(axis)
    return lax.ppermute(x, axis, [(i, (i + by) % size) for i in range(size)])


def sent_to_all(x, axis):
    size = lax.axis_size(axis)
    return lax.all_to_all(jnp.broadcast_to(x[None], (size, *x.shape)), axis, 0, 0, tiled=True)


def of_everyone(x, axis):
    return sent_to_all(x, axis).sum(axis=0)


def in_one(arrays, axis):
    ends = [0]
    for a in arrays:
        ends.append(ends[-1] + a.size)
    subtotal = of_everyone(jnp.concatenate([a.ravel() for a in arrays]), axis)
    return tuple((subtotal[b:e].reshape(a.shape) for a, b, e in zip(arrays, ends, ends[1:])))


def cut_along(x, dim, size):
    before, after = (x.shape[:dim], x.shape[dim + 1 :])
    return jnp.moveaxis(x.reshape(*before, size, -1, *after), dim, 0)


def sum_at_owner(x, axis, dim):
    pieces = cut_along(x, dim, lax.axis_size(axis))
    arrived = lax.all_to_all(pieces, axis, split_axis=0, concat_axis=0, tiled=True)
    return arrived.sum(axis=0)


def joined_along(pieces, dim):
    dims = list(pieces.shape[1:])
    dims[dim] *= pieces.shape[0]
    return jnp.moveaxis(pieces, 0, dim).reshape(dims)


def gathered_copies(x, axis, dim):
    return joined_along(sent_to_all(x, axis), dim)


def shards(stream, expert_ids, norm_gain, router, w_up, w_down):
    ahead = shifted(stream[0], "pipe", 1)
    behind = shifted(stream[1], "pipe", -1)
    arrived = jnp.concatenate([ahead, behind], axis=0).astype(jnp.float32)
    tok_rows = arrived.shape[1]
    quarter = arrived.shape[2]
    width = float(quarter * lax.axis_size("tensor"))
    scaled = arrived * norm_gain[0]
    squares = jnp.sum(arrived * arrived, axis=-1)
    highest = lax.Precision.HIGHEST
    total_sq, partial_value = in_one(
        (squares, jnp.einsum("dtc,ce->dte", scaled, router[0], precision=highest)), "tensor"
    )
    inverse = lax.rsqrt(total_sq / width + norm_eps)
    normed = scaled * inverse[..., None]
    logits = partial_value * inverse[..., None]
    chosen = expert_ids[:, 0]
    fanout = chosen.shape[2]
    experts = router.shape[2]
    capacity = 3 * tok_rows * fanout // (2 * experts)
    picked = jnp.take_along_axis(logits, chosen, axis=-1)
    scores = jax.nn.sigmoid(picked)
    gates = route_scale * scores / jnp.sum(scores, axis=-1, keepdims=True)
    onehot = (chosen[..., None] == jnp.arange(experts, dtype=jnp.int32)).astype(jnp.int32)
    onehot = onehot.reshape(2, tok_rows * fanout, experts)
    earlier = jnp.cumsum(onehot, axis=1) - onehot
    within = jnp.sum(earlier * onehot, axis=-1).reshape(chosen.shape)
    heading = lax.broadcasted_iota(jnp.int32, chosen.shape, 0)
    member = lax.broadcasted_iota(jnp.int32, chosen.shape, 1)
    target = chosen * (2 * capacity) + heading * capacity + within
    anchor = heading * tok_rows + member
    owner = (
        jnp.full((experts * 2 * capacity,), 2 * tok_rows, jnp.int32)
        .at[target.reshape(-1)]
        .set(anchor.reshape(-1))
    )
    hidden = normed.astype(jnp.bfloat16).reshape(2 * tok_rows, quarter)
    table = jnp.concatenate([hidden, jnp.zeros((1, quarter), jnp.bfloat16)], axis=0)
    outgoing = table[owner].reshape(experts, 2 * capacity, quarter)
    upper = w_up[0]
    lower = w_down[0]
    received = lax.all_to_all(outgoing, "expert", split_axis=0, concat_axis=0, tiled=True)
    senders = received.shape[0]
    count = received.shape[1]
    inner = jnp.dot(received.reshape(-1, quarter), upper, preferred_element_type=jnp.float32)
    share = sum_at_owner(inner, "tensor", 1)
    active = gathered_copies(jax.nn.silu(share).astype(jnp.bfloat16), "tensor", 1)
    produced = jnp.dot(active, lower, preferred_element_type=jnp.float32).astype(jnp.bfloat16)
    answers = lax.all_to_all(
        produced.reshape(senders, count, quarter), "expert", split_axis=0, concat_axis=0, tiled=True
    )
    flat_back = answers.reshape(experts * 2 * capacity, quarter)
    gathered = (
        flat_back[target.reshape(-1)].reshape(2, tok_rows, fanout, quarter).astype(jnp.float32)
    )
    mixed = jnp.einsum("dtk,dtkc->dtc", gates, gathered)
    result = (arrived + mixed).astype(jnp.bfloat16)
    return result[:, None]


def solution(mesh):
    return jax.shard_map(
        shards,
        mesh=mesh,
        in_specs=(
            P(None, "pipe", "expert", "tensor"),
            P(None, "pipe", "expert", None),
            P("pipe", "tensor"),
            P("pipe", "tensor", None),
            P("expert", "tensor", None),
            P("expert", None, "tensor"),
        ),
        out_specs=P(None, "pipe", "expert", "tensor"),
        check_vma=False,
    )
```

profile of v0, /device:TPU:1, one launch (start us, length us, event | category | flops | bytes accessed | tf_op | source)
XLA Modules:
  0.0 231.8 jit_solution(7772980050450476414)
XLA Ops:
  0.0 0.0 copy-start
  0.0 0.9 slice_bitcast_fusion.1
  0.9 9.3 %collective-permute-start = (bf16[1,16,1792]{2,1,0:T(8,128)(2,1)S(1)}, bf16[1,16,1792]{2,1,0:T(8,128)(2,1)S(1)}, u32[]{:S(2)}, u32[]{:S(2)}) collective-permute-start(bf16[1,16,1792]{2,1,0:T(8,128)(2,1)S(1)} %get-tuple-element.7), channel_id=1, source_target_pairs={{0,256},{256,512},{512,768},{768,0},{1,257},{257,513},{513,769},{7... | collective-permute-start | bytes 172040 | tf_op jit(solution)/shard_map/ppermute | solution.py:12
  10.2 8.7 %collective-permute-start.1 = (bf16[1,16,1792]{2,1,0:T(8,128)(2,1)S(1)}, bf16[1,16,1792]{2,1,0:T(8,128)(2,1)S(1)}, u32[]{:S(2)}, u32[]{:S(2)}) collective-permute-start(bf16[1,16,1792]{2,1,0:T(8,128)(2,1)S(1)} %get-tuple-element.8), channel_id=1, source_target_pairs={{0,768},{256,0},{512,256},{768,512},{1,769},{257,1},{513,257},{769... | collective-permute-start | bytes 172040 | tf_op jit(solution)/shard_map/ppermute | solution.py:12
  18.9 0.8 copy.25
  19.6 0.7 broadcast_multiply_fusion.1
  20.3 0.1 eq.16
  20.4 0.1 fusion.12
  20.5 0.2 reduce_window_sum.11
  20.7 0.2 select_reduce_fusion
  20.9 0.1 copy.28
  21.0 0.1 mul.97
  21.1 0.1 iota.24
  21.2 0.1 iota.25
  21.3 0.1 iota_add_fusion
  21.3 0.1 reshape.202
  21.4 1.4 scatter_custom_fusion
  22.9 0.7 reduce.1
  23.6 0.0 collective-permute-done
  23.6 0.0 collective-permute-done.1
  23.6 0.0 copy-done
  23.6 0.5 fusion.5
  24.1 0.1 reshape.166
  24.2 0.1 multiply_reduce_fusion
  24.3 0.1 reshape.165
  24.4 0.1 pad_maximum_fusion.1
  24.4 0.6 broadcast_in_dim.14
  25.1 3.3 %all-to-all-start = ((f32[4,1,2080]{2,1,0:T(1,128)}), f32[4,1,2080]{2,1,0:T(1,128)S(1)}, u32[]{:S(2)}, u32[]{:S(2)}) async-start(f32[4,1,2080]{2,1,0:T(1,128)} %broadcast_in_dim.14), calls=%async_computation | async-start | bytes 69632 | tf_op jit(solution)/shard_map/all_to_all | solution.py:17
  28.4 4.5 %all-to-all-done = f32[4,1,2080]{2,1,0:T(1,128)S(1)} async-done(((f32[4,1,2080]{2,1,0:T(1,128)}), f32[4,1,2080]{2,1,0:T(1,128)S(1)}, u32[]{:S(2)}, u32[]{:S(2)}) %all-to-all-start) | async-done | bytes 33312 | tf_op jit(solution)/shard_map/all_to_all | solution.py:17
  32.9 0.1 fusion.9
  33.0 2.4 %gather_fusion = bf16[384,1792]{1,0:T(8,128)(2,1)S(1)} fusion(bf16[33,1792]{1,0:T(8,128)(2,1)S(1)} %concatenate.11, s32[1024]{0:T(1024)S(1)} %pad_clamp_fusion.1), kind=kCustom, calls=%fused_computation | custom fusion | bytes 2754048 | tf_op jit(solution)/shard_map/gather | solution.py:91
  35.4 1.5 reshape.169
  36.9 18.7 %all-to-all-start.1 = ((bf16[64,6,1792]{2,1,0:T(8,128)(2,1)}), bf16[64,6,1792]{2,1,0:T(8,128)(2,1)S(1)}, u32[]{:S(2)}, u32[]{:S(2)}) async-start(bf16[64,6,1792]{2,1,0:T(8,128)(2,1)} %reshape.169), calls=%async_computation.1 | async-start | bytes 3670016 | tf_op jit(solution)/shard_map/all_to_all | solution.py:94
  55.6 6.0 %copy.34 = bf16[1024,1792]{1,0:T(8,128)(2,1)} copy(bf16[1024,1792]{0,1:T(8,128)(2,1)} %bitcast.67) | data formatting | bytes 7340032 | tf_op jit(solution)/shard_map/dot_general | solution.py:97
  61.6 39.7 %all-to-all-done.1 = bf16[64,6,1792]{2,1,0:T(8,128)(2,1)S(1)} async-done(((bf16[64,6,1792]{2,1,0:T(8,128)(2,1)}), bf16[64,6,1792]{2,1,0:T(8,128)(2,1)S(1)}, u32[]{:S(2)}, u32[]{:S(2)}) %all-to-all-start.1) | async-done | bytes 1376288 | tf_op jit(solution)/shard_map/all_to_all | solution.py:94
  101.3 1.3 reshape.208
  102.6 4.1 %convolution_bitcast_fusion = f32[4,384,256]{2,1,0:T(8,128)S(1)} fusion(bf16[384,1792,1]{1,0,2:T(8,128)(2,1)} %reshape.208, bf16[4,256,1792]{2,1,0:T(8,128)(2,1)} %bitcast.68), kind=kOutput, calls=%fused_computation.7 | convolution fusion | flops 1409286144 | bytes 6619136 | tf_op jit(solution)/shard_map/dot_general | solution.py:97
  106.7 38.4 %all_to_all.26 = f32[4,384,256]{2,1,0:T(8,128)S(1)} all-to-all(f32[4,384,256]{2,1,0:T(8,128)S(1)} %convolution_bitcast_fusion), channel_id=1, replica_groups=mesh['pipe'=4,'expert'=64,'tensor'=4] {'tensor'}, dimensions={0} | all-to-all | bytes 3145728 | tf_op jit(solution)/shard_map/all_to_all | solution.py:39
  145.0 0.1 reduce_sum.49
  145.2 0.1 multiply_convert_fusion
  145.3 0.2 copy.31
  145.4 0.1 broadcast_in_dim.18
  145.5 21.7 %all_to_all.27 = bf16[4,384,256]{1,2,0:T(8,128)(2,1)S(1)} all-to-all(bf16[4,384,256]{1,2,0:T(8,128)(2,1)S(1)} %broadcast_in_dim.18), channel_id=1, replica_groups=mesh['pipe'=4,'expert'=64,'tensor'=4] {'tensor'}, dimensions={0} | all-to-all | bytes 1572864 | tf_op jit(solution)/shard_map/all_to_all | solution.py:17
  167.2 3.7 %fusion.2 = bf16[384,1792]{1,0:T(8,128)(2,1)S(1)} fusion(bf16[384,1024]{0,1:T(8,128)(2,1)S(1)} %bitcast.69, bf16[1,1024,1792]{2,1,0:T(8,128)(2,1)} %param.11), kind=kOutput, calls=%fused_computation.6 | convolution fusion | flops 1409974272 | bytes 5832704 | tf_op jit(solution)/shard_map/dot_general | solution.py:100
  170.9 1.5 reshape.172
  172.4 0.0 copy-start.1
  172.4 11.5 %all-to-all-start.4 = ((bf16[64,6,1792]{2,1,0:T(8,128)(2,1)}), bf16[64,6,1792]{2,1,0:T(8,128)(2,1)}, u32[]{:S(2)}, u32[]{:S(2)}) async-start(bf16[64,6,1792]{2,1,0:T(8,128)(2,1)} %reshape.172), calls=%async_computation.4 | async-start | bytes 3670016 | tf_op jit(solution)/shard_map/all_to_all | solution.py:101
  183.9 0.0 copy-done.1
  183.9 0.1 copy.27
  184.0 0.1 reshape.192
  184.1 0.1 rsqrt.12
  184.2 0.1 slice.31
  184.3 0.1 reshape.167
  184.3 0.1 broadcast_multiply_fusion
  184.4 2.4 %gather_fusion.2 = f32[256]{0:T(256)S(1)} fusion(f32[2,16,64]{2,1,0:T(8,128)S(1)} %broadcast_multiply_fusion, s32[256]{0:T(256)S(1)} %reshape.192), kind=kCustom, calls=%fused_computation.2 | custom fusion | bytes 5120 | tf_op jit(solution)/shard_map/jit(take_along_axis)/gather | solution.py:73
  186.9 0.1 reshape.195
  186.9 0.1 fusion.22
  187.1 0.1 multiply_divide_fusion
  187.1 39.9 %all-to-all-done.4 = bf16[64,6,1792]{2,1,0:T(8,128)(2,1)} async-done(((bf16[64,6,1792]{2,1,0:T(8,128)(2,1)}), bf16[64,6,1792]{2,1,0:T(8,128)(2,1)}, u32[]{:S(2)}, u32[]{:S(2)}) %all-to-all-start.4) | async-done | bytes 1376288 | tf_op jit(solution)/shard_map/all_to_all | solution.py:101
  227.0 2.4 %reshape.173 = bf16[384,1792]{1,0:T(8,128)(2,1)S(1)} reshape(bf16[64,6,1792]{2,1,0:T(8,128)(2,1)} %all-to-all-done.4) | data formatting | bytes 2752512 | tf_op jit(solution)/shard_map/reshape | solution.py:104
  229.4 1.3 gather_fusion.1
  230.8 0.4 fusion.23
  231.2 0.7 fusion.13
  (10 shorter events, 0.1 us)
Async XLA Ops:
  0.0 23.6 %copy-start = (f32[1,1792,64]{1,2,0:T(8,128)S(1)}, f32[1,1792,64]{1,2,0:T(8,128)}, u32[]{:S(2)}) copy-start(f32[1,1792,64]{1,2,0:T(8,128)} %param.9) | copy-start | bytes 1376260
  0.9 22.7 %collective-permute-start = (bf16[1,16,1792]{2,1,0:T(8,128)(2,1)S(1)}, bf16[1,16,1792]{2,1,0:T(8,128)(2,1)S(1)}, u32[]{:S(2)}, u32[]{:S(2)}) collective-permute-start(bf16[1,16,1792]{2,1,0:T(8,128)(2,1)S(1)} %get-tuple-element.7), channel_id=1, source_target_pairs={{0,256},{256,512},{512,768},{768,0},{1,257},{257,513},{513,769},{7... | collective-permute-start | bytes 172040 | tf_op jit(solution)/shard_map/ppermute | solution.py:12
  10.2 13.4 %collective-permute-start.1 = (bf16[1,16,1792]{2,1,0:T(8,128)(2,1)S(1)}, bf16[1,16,1792]{2,1,0:T(8,128)(2,1)S(1)}, u32[]{:S(2)}, u32[]{:S(2)}) collective-permute-start(bf16[1,16,1792]{2,1,0:T(8,128)(2,1)S(1)} %get-tuple-element.8), channel_id=1, source_target_pairs={{0,768},{256,0},{512,256},{768,512},{1,769},{257,1},{513,257},{769... | collective-permute-start | bytes 172040 | tf_op jit(solution)/shard_map/ppermute | solution.py:12
  25.1 7.8 %all-to-all-start = ((f32[4,1,2080]{2,1,0:T(1,128)}), f32[4,1,2080]{2,1,0:T(1,128)S(1)}, u32[]{:S(2)}, u32[]{:S(2)}) async-start(f32[4,1,2080]{2,1,0:T(1,128)} %broadcast_in_dim.14), calls=%async_computation | async-start | bytes 69632 | tf_op jit(solution)/shard_map/all_to_all | solution.py:17
  36.9 64.4 %all-to-all-start.1 = ((bf16[64,6,1792]{2,1,0:T(8,128)(2,1)}), bf16[64,6,1792]{2,1,0:T(8,128)(2,1)S(1)}, u32[]{:S(2)}, u32[]{:S(2)}) async-start(bf16[64,6,1792]{2,1,0:T(8,128)(2,1)} %reshape.169), calls=%async_computation.1 | async-start | bytes 3670016 | tf_op jit(solution)/shard_map/all_to_all | solution.py:94
  172.4 11.5 %copy-start.1 = (s32[2,1,16,8]{2,3,1,0:T(8,128)S(1)}, s32[2,1,16,8]{2,3,1,0:T(8,128)}, u32[]{:S(2)}) copy-start(s32[2,1,16,8]{2,3,1,0:T(8,128)} %param.7) | copy-start | bytes 3076
  172.4 54.6 %all-to-all-start.4 = ((bf16[64,6,1792]{2,1,0:T(8,128)(2,1)}), bf16[64,6,1792]{2,1,0:T(8,128)(2,1)}, u32[]{:S(2)}, u32[]{:S(2)}) async-start(bf16[64,6,1792]{2,1,0:T(8,128)(2,1)} %reshape.172), calls=%async_computation.4 | async-start | bytes 3670016 | tf_op jit(solution)/shard_map/all_to_all | solution.py:101
where the time goes:
time: 235 us; the launch traced here: 232 us
  waiting for transfers between devices  84 us (36%)
  blocking collectives  60.1 us (26%)
  starting transfers between devices  51.4 us (22%)
  local copies, waits for them, and re-layouts  24 us (10%)
  matrix products  8.6 us (4%)
  other arithmetic  3.48 us (1%)
    all_to_all x1, waiting for transfers between devices, shards(): lax.all_to_all(produced.reshape(senders, count, quarter), 'expert', split...  39.9 us
    all_to_all x1, waiting for transfers between devices, shards(): lax.all_to_all(outgoing, 'expert', split_axis=0, concat_axis=0, tiled=True)  39.7 us
    all_to_all x1, blocking collectives, sum_at_owner(): lax.all_to_all(pieces, axis, split_axis=0, concat_axis=0, tiled=True)  38.4 us
    all_to_all x1, blocking collectives, sent_to_all(): lax.all_to_all(jnp.broadcast_to(x[None], (size, *x.shape)), axis, 0, 0, t...  21.7 us
    all_to_all x1, starting transfers between devices, shards(): lax.all_to_all(outgoing, 'expert', split_axis=0, concat_axis=0, tiled=True)  18.7 us
    ppermute x2, starting transfers between devices, shifted(): return lax.ppermute(x, axis, [(i, (i + by) % size) for i in range(size)])  17.9 us
    all_to_all x1, starting transfers between devices, shards(): lax.all_to_all(produced.reshape(senders, count, quarter), 'expert', split...  11.5 us
    dot_general x1, local copies, waits for them, and re-layouts, shards(): jnp.dot(received.reshape(-1, quarter), upper, preferred_element_type=jnp....  5.98 us
  transfers between devices with their start and end apart: 5, of which 3 were waited for; matrix products, arithmetic and copies ran while one was open for 6% of the time, Pallas kernels for 0%

commit v1 on v0

v1 whole, which is shorter than its diff:
```python
import functools

import jax
import jax.numpy as jnp
from jax import lax
from jax.experimental import pallas as pl
from jax.experimental.pallas import tpu as pltpu
from jax.sharding import PartitionSpec as P

norm_eps = 1e-06
route_scale = 2.5
MESH = pl.DeviceIdType.MESH
BF = jnp.bfloat16
F32 = jnp.float32
LANES = 128


def over(v, n, limit):
    m = -(-65536 // n)
    assert all((i * m) >> 16 == i // n for i in range(limit))
    return (v * m) >> 16


def split3(v):
    hi = v.astype(BF)
    rest = v - hi.astype(F32)
    mid = rest.astype(BF)
    low = (rest - mid.astype(F32)).astype(BF)
    return hi, mid, low


def nt_dot(a, b):
    return lax.dot_general(a, b, (((1,), (1,)), ((), ())), preferred_element_type=F32)


def mm(a, b):
    return jnp.dot(a, b, preferred_element_type=F32)


def layer(
    cfg, stream, ids, gain, router, w_up, w_down, out,
    up, down, rparts, arr, blocks, codes, info, stat_s, stat_r, sel_s, rows, part_s, part_r, own_part,
    act, made_s, made_r, mix_s, mix_r,
    w_sem, shift_ss, shift_rs, code_ss, code_rs, block_ss, block_rs, info_ss, info_rs, stat_ss, stat_rs,
    sel_ss, sel_rs, part_ss, part_rs, act_ss, act_rs, made_ss, made_rs, mix_ss, mix_rs,
):
    np_, nz, nx, nt, tok, cap, experts, width = cfg
    quarter = stream.shape[-1]
    ff = w_up.shape[-1]
    fq = ff // nt
    p = lax.axis_index("pipe")
    e = lax.axis_index("expert")
    t = lax.axis_index("tensor")
    z, x = e // nx, e % nx
    n1, n2 = (nx, nz), (nz, nx)
    c1, c2 = (x, z), (z, x)

    def at1(d, j):
        return z * nx + j if d == 0 else j * nx + x

    def at2(d, j):
        return j * nx + x if d == 0 else z * nx + j

    def to_expert(j):
        return {"expert": j}

    started = []

    def copy(src, dst, ss, rs, dev):
        c = pltpu.make_async_remote_copy(
            src_ref=src, dst_ref=dst, send_sem=ss, recv_sem=rs, device_id=dev, device_id_type=MESH
        )
        return c

    def send(*a):
        c = copy(*a)
        c.start()
        started.append(c)

    cu = pltpu.make_async_copy(w_up, up, w_sem.at[0])
    cd = pltpu.make_async_copy(w_down, down, w_sem.at[1])
    cu.start()
    cd.start()

    barrier = pltpu.get_barrier_semaphore()
    peers = [{"pipe": lax.rem(p + 1, np_)}, {"pipe": lax.rem(p + np_ - 1, np_)}]
    peers += [to_expert(at1(0, lax.rem(x + k, nx))) for k in range(1, nx)]
    peers += [to_expert(at2(0, lax.rem(z + k, nz))) for k in range(1, nz)]
    peers += [{"tensor": lax.rem(t + k, nt)} for k in range(1, nt)]
    for dev in peers:
        pl.semaphore_signal(barrier, inc=1, device_id=dev, device_id_type=MESH)

    lane = lax.broadcasted_iota(jnp.int32, (tok, LANES), 1)
    before = (
        lax.broadcasted_iota(jnp.int32, (tok, tok), 0) > lax.broadcasted_iota(jnp.int32, (tok, tok), 1)
    ).astype(F32)
    named = []
    for d in range(2):
        chosen = ids[d, 0]
        hot = jnp.zeros((tok, LANES), F32)
        for k in range(chosen.shape[1]):
            hot = hot + (chosen[:, k : k + 1] == lane).astype(F32)
        named.append(hot)
        earlier = mm(before.astype(BF), hot.astype(BF))
        codes[d, c1[d]] = (hot * (earlier + 1.0)).astype(BF)
    for i, part in enumerate(split3(router[0])):
        rparts[:, i * experts : (i + 1) * experts] = part

    pl.semaphore_wait(barrier, len(peers))

    for d in range(2):
        dev = {"pipe": lax.rem(p + (1 if d == 0 else np_ - 1), np_)}
        send(stream.at[d, 0], arr.at[d], shift_ss.at[d], shift_rs.at[d], dev)
    for d in range(2):
        for k in range(1, n1[d]):
            j = lax.rem(c1[d] + k, n1[d])
            here = codes.at[d, c1[d]]
            send(here, here, code_ss.at[d, k], code_rs.at[d, k], to_expert(at1(d, j)))
    for d in range(2):
        copy(stream.at[d, 0], arr.at[d], shift_ss.at[d], shift_rs.at[d], {"pipe": p}).wait_recv()
        for k in range(1, n1[d]):
            j = lax.rem(c1[d] + k, n1[d])
            send(arr.at[d], blocks.at[d, c1[d]], block_ss.at[d, k], block_rs.at[d, k], to_expert(at1(d, j)))
        blocks[d, c1[d]] = arr[d]

    both = jnp.concatenate([arr[0], arr[1]], axis=0).astype(F32)
    squares = jnp.sum(both * both, axis=-1, keepdims=True)
    scaled = both * gain[...]
    hi, mid, low = split3(scaled)
    n = 2 * tok
    prod = mm(jnp.concatenate([hi, mid, low], axis=0), rparts[...])
    r0, r1, r2 = (slice(i * experts, (i + 1) * experts) for i in range(3))
    small = prod[2 * n :, r0] + prod[n : 2 * n, r1] + prod[:n, r2]
    partial = prod[:n, r0] + (prod[:n, r1] + prod[n : 2 * n, r0] + small)
    stat_s[:, :experts] = partial
    stat_s[:, experts:] = jnp.broadcast_to(squares, (n, LANES - experts))
    for k in range(1, nt):
        send(stat_s, stat_r.at[k], stat_ss.at[k], stat_rs.at[k], {"tensor": lax.rem(t + k, nt)})
    total = stat_s[...]
    for k in range(1, nt):
        copy(stat_s, stat_r.at[k], stat_ss.at[k], stat_rs.at[k], {"tensor": t}).wait_recv()
        total = total + stat_r[k]
    inverse = lax.rsqrt(total[:, experts : experts + 1] / width + norm_eps)
    hot = jnp.concatenate(named, axis=0)
    scores = jax.nn.sigmoid(total * inverse) * hot
    gates = route_scale * scores / jnp.sum(scores, axis=-1, keepdims=True)
    lane2 = lax.broadcasted_iota(jnp.int32, (n, LANES), 1)
    both_info = jnp.where(lane2 < experts, gates, jnp.broadcast_to(inverse, (n, LANES)))
    for d in range(2):
        info[d, c1[d]] = both_info[d * tok : (d + 1) * tok]
        for k in range(1, n1[d]):
            j = lax.rem(c1[d] + k, n1[d])
            here = info.at[d, c1[d]]
            send(here, here, info_ss.at[d, k], info_rs.at[d, k], to_expert(at1(d, j)))

    weights = []
    for d in range(2):
        a, b = n1[d], n2[d]
        nr, nc, per = a * b * cap, a * tok, a * cap
        for k in range(1, a):
            j = lax.rem(c1[d] + a - k, a)
            copy(codes.at[d, j], codes.at[d, j], code_ss.at[d, k], code_rs.at[d, k], to_expert(e)).wait_recv()
        code = codes[d].reshape(nc, LANES)
        rr = lax.broadcasted_iota(jnp.int32, (nr, LANES), 0)
        at = at2(d, over(rr, per, nr))
        pick = (lax.broadcasted_iota(jnp.int32, (nr, LANES), 1) == at).astype(F32).astype(BF)

        def chosen_of(shape, rdim, value):
            r = lax.broadcasted_iota(jnp.int32, shape, rdim)
            c = lax.broadcasted_iota(jnp.int32, shape, 1 - rdim)
            third = over(r, cap, nr)
            slot = r - third * cap
            block = third - over(r, per, nr) * a
            return (value == (slot + 1).astype(F32)) & (block == over(c, tok, nc))

        sel = chosen_of((nr, nc), 0, nt_dot(pick, code)).astype(F32).astype(BF)
        keep = chosen_of((nc, nr), 1, nt_dot(code, pick))
        for k in range(1, a):
            j = lax.rem(c1[d] + a - k, a)
            copy(info.at[d, j], info.at[d, j], info_ss.at[d, k], info_rs.at[d, k], to_expert(e)).wait_recv()
        facts = info[d].reshape(nc, LANES)
        ghi = facts.astype(BF)
        glo = (facts - ghi.astype(F32)).astype(BF)
        whi = jnp.where(keep, nt_dot(ghi, pick), 0.0).astype(BF)
        wlo = jnp.where(keep, nt_dot(glo, pick), 0.0).astype(BF)
        weights.append((whi, wlo))
        for k in range(1, a):
            j = lax.rem(c1[d] + a - k, a)
            copy(arr.at[d], blocks.at[d, j], block_ss.at[d, k], block_rs.at[d, k], to_expert(e)).wait_recv()
        inv = facts[:, experts : experts + 1]
        hidden = (blocks[d].reshape(nc, quarter).astype(F32) * gain[...] * inv).astype(BF)
        picked = mm(sel, hidden)
        for j in range(b):
            sel_s[d, j] = picked[j * per : (j + 1) * per].astype(BF)
        for k in range(1, b):
            j = lax.rem(c2[d] + k, b)
            send(sel_s.at[d, j], rows.at[d, c2[d]], sel_ss.at[d, k], sel_rs.at[d, k], to_expert(at2(d, j)))
        rows[d, c2[d]] = sel_s[d, c2[d]]

    cu.wait()
    for d in range(2):
        a, b = n1[d], n2[d]
        nr = a * b * cap
        for k in range(1, b):
            j = lax.rem(c2[d] + b - k, b)
            copy(sel_s.at[d, j], rows.at[d, j], sel_ss.at[d, k], sel_rs.at[d, k], to_expert(e)).wait_recv()
        lhs = rows[d].reshape(nr, quarter)
        for k in list(range(1, nt)) + [0]:
            q = lax.rem(t + k, nt)
            part = mm(lhs, up[:, pl.ds(pl.multiple_of(q * fq, fq), fq)])
            if k:
                part_s[d, k] = part.astype(BF)
                send(part_s.at[d, k], part_r.at[d, k], part_ss.at[d, k], part_rs.at[d, k], {"tensor": q})
            else:
                own_part[d] = part
    for d in range(2):
        inner = own_part[d]
        for k in range(1, nt):
            copy(part_s.at[d, k], part_r.at[d, k], part_ss.at[d, k], part_rs.at[d, k], {"tensor": t}).wait_recv()
            inner = inner + part_r[d, k].astype(F32)
        act[d, t] = jax.nn.silu(inner).astype(BF)
        for k in range(1, nt):
            q = lax.rem(t + k, nt)
            send(act.at[d, t], act.at[d, t], act_ss.at[d, k], act_rs.at[d, k], {"tensor": q})
    cd.wait()
    for d in range(2):
        a, b = n1[d], n2[d]
        per = a * cap
        for k in range(1, nt):
            q = lax.rem(t + nt - k, nt)
            copy(act.at[d, q], act.at[d, q], act_ss.at[d, k], act_rs.at[d, k], {"tensor": t}).wait_recv()
        lhs = jnp.concatenate([act[d, q] for q in range(nt)], axis=1)
        step = min(256, quarter)
        for s in range(0, quarter, step):
            made = mm(lhs, down[:, s : s + step])
            for j in range(b):
                made_s[d, j, :, s : s + step] = made[j * per : (j + 1) * per].astype(BF)
        for k in range(1, b):
            j = lax.rem(c2[d] + k, b)
            send(made_s.at[d, j], made_r.at[d, c2[d]], made_ss.at[d, k], made_rs.at[d, k], to_expert(at2(d, j)))
        made_r[d, c2[d]] = made_s[d, c2[d]]

    for d in range(2):
        a, b = n1[d], n2[d]
        nr = a * b * cap
        for k in range(1, b):
            j = lax.rem(c2[d] + b - k, b)
            copy(made_s.at[d, j], made_r.at[d, j], made_ss.at[d, k], made_rs.at[d, k], to_expert(e)).wait_recv()
        back = made_r[d].reshape(nr, quarter)
        whi, wlo = weights[d]
        mixed = mm(whi, back) + mm(wlo, back)
        for j in range(a):
            mix_s[d, j] = mixed[j * tok : (j + 1) * tok].astype(BF)
        for k in range(1, a):
            j = lax.rem(c1[d] + k, a)
            send(mix_s.at[d, j], mix_r.at[d, k], mix_ss.at[d, k], mix_rs.at[d, k], to_expert(at1(d, j)))
    for d in range(2):
        total = mix_s[d, c1[d]].astype(F32)
        for k in range(1, n1[d]):
            copy(mix_s.at[d, 0], mix_r.at[d, k], mix_ss.at[d, k], mix_rs.at[d, k], to_expert(e)).wait_recv()
            total = total + mix_r[d, k].astype(F32)
        out[d, 0] = (arr[d].astype(F32) + total).astype(BF)
    for c in started:
        c.wait_send()


def solution(mesh, nz=8, nx=8, cap=3):
    np_, nt = mesh.shape["pipe"], mesh.shape["tensor"]

    def shards(stream, ids, gain, router, w_up, w_down):
        tok, quarter = stream.shape[2:]
        experts, ff = router.shape[2], w_up.shape[2]
        cfg = (np_, nz, nx, nt, tok, cap, experts, float(quarter * nt))
        big, per = max(nz, nx), (nx * cap, nz * cap)
        assert nx == nz
        nr, fq = nx * nz * cap, ff // nt
        V, S = pltpu.VMEM, pltpu.SemaphoreType.DMA
        whole = pl.BlockSpec(memory_space=V)
        far = pl.BlockSpec(memory_space=pl.ANY)
        vmem = [
            V((quarter, ff), BF), V((ff, quarter), BF), V((quarter, 3 * experts), BF),
            V((2, tok, quarter), BF), V((2, big, tok, quarter), BF), V((2, big, tok, LANES), BF), V((2, big, tok, LANES), F32),
            V((2 * tok, LANES), F32), V((nt, 2 * tok, LANES), F32),
            V((2, big, per[0], quarter), BF), V((2, big, per[0], quarter), BF),
            V((2, nt, nr, fq), BF), V((2, nt, nr, fq), BF), V((2, nr, fq), F32), V((2, nt, nr, fq), BF),
            V((2, big, per[0], quarter), BF), V((2, big, per[0], quarter), BF),
            V((2, big, tok, quarter), BF), V((2, big, tok, quarter), BF),
        ]
        sems = [S((2,)), S((2,)), S((2,))] + [S((2, big))] * 6 + [S((nt,))] * 2 + [S((2, big))] * 2 + [S((2, nt))] * 4 + [S((2, big))] * 4
        return pl.pallas_call(
            functools.partial(layer, cfg),
            out_shape=jax.ShapeDtypeStruct(stream.shape, BF),
            in_specs=[whole] * 4 + [far] * 2,
            out_specs=whole,
            scratch_shapes=vmem + sems,
            compiler_params=pltpu.CompilerParams(
                collective_id=0, has_side_effects=True, vmem_limit_bytes=48 * 1024 * 1024
            ),
        )(stream, ids, gain, router, w_up[0], w_down[0])

    return jax.shard_map(
        shards,
        mesh=mesh,
        in_specs=(
            P(None, "pipe", "expert", "tensor"),
            P(None, "pipe", "expert", None),
            P("pipe", "tensor"),
            P("pipe", "tensor", None),
            P("expert", "tensor", None),
            P("expert", None, "tensor"),
        ),
        out_specs=P(None, "pipe", "expert", "tensor"),
        check_vma=False,
    )
```

time: 235 us -> 133 us (0.57)
  Pallas kernels: 0 us -> 125 us
  waiting for transfers between devices: 84 us -> 0 us
  blocking collectives: 60.1 us -> 0 us
  starting transfers between devices: 51.4 us -> 0 us
  local copies, waits for them, and re-layouts: 24 us -> 6.36 us
  matrix products: 8.6 us -> 0 us
  other arithmetic: 3.48 us -> 0 us
    pallas_call x0 -> x1, Pallas kernels: none -> 125 us  [shards(): pl.pallas_call(functools.partial(layer, cfg), out_shape=jax.ShapeDtypeStr...]
    all_to_all x3 -> x0, waiting for transfers between devices: 84 us -> none  [the longest x1 39.9 us: shards(): lax.all_to_all(produced.reshape(senders, count, quarter), 'expert', split...]
    all_to_all x2 -> x0, blocking collectives: 60.1 us -> none  [the longest x1 38.4 us: sum_at_owner(): lax.all_to_all(pieces, axis, split_axis=0, concat_axis=0, tiled=True)]
    all_to_all x3 -> x0, starting transfers between devices: 33.5 us -> none  [the longest x1 18.7 us: shards(): lax.all_to_all(outgoing, 'expert', split_axis=0, concat_axis=0, tiled=True)]
    ppermute x2 -> x0, starting transfers between devices: 17.9 us -> none  [shifted(): return lax.ppermute(x, axis, [(i, (i + by) % size) for i in range(size)])]
    dot_general x4 -> x0, matrix products: 8.6 us -> none  [the longest x1 4.06 us: shards(): jnp.dot(received.reshape(-1, quarter), upper, preferred_element_type=jnp....]
    reshape x7 -> x0, local copies, waits for them, and re-layouts: 6.96 us -> none  [the longest x1 2.44 us: shards(): flat_back = answers.reshape(experts * 2 * capacity, quarter)]
    gather x6 -> x0, local copies, waits for them, and re-layouts: 6.4 us -> none  [the longest x4 2.69 us: shards(): picked = jnp.take_along_axis(logits, chosen, axis=-1)]
  transfers between devices with their start and end apart: 5 -> 0, of which waited for: 3 -> 0; matrix products, arithmetic and copies ran while one was open for 6% -> 0% of each run, Pallas kernels for 0% -> 0%
where the time goes in v1:
time: 133 us; the launch traced here: 131 us
  Pallas kernels  125 us (94%)
  local copies, waits for them, and re-layouts  6.36 us (5%)
    pallas_call x1, Pallas kernels, shards(): pl.pallas_call(functools.partial(layer, cfg), out_shape=jax.ShapeDtypeStr...  125 us
    unnamed x9, local copies, waits for them, and re-layouts  6.36 us

profile of v1, /device:TPU:1, one launch (start us, length us, event | category | flops | bytes accessed | tf_op | source)
XLA Modules:
  0.0 130.9 jit_solution(10218674998619251663)
XLA Ops:
  0.0 0.8 copy.7.ids
  0.8 1.3 %copy.8.router = f32[1,1792,64]{2,1,0:T(8,128)S(1)} copy(f32[1,1792,64]{1,2,0:T(8,128)} %param.9) | data formatting | bytes 917504 | tf_op args[3]
  2.1 0.0 copy-start
  2.1 2.0 %copy-done = bf16[1,1792,1024]{2,1,0:T(8,128)(2,1)S(1)} copy-done((bf16[1,1792,1024]{2,1,0:T(8,128)(2,1)S(1)}, bf16[1,1792,1024]{2,1,0:T(8,128)(2,1)}, u32[]{:S(2)}) %copy-start) | copy-done | bytes 3670040
  4.1 0.0 copy-start.1
  4.1 0.9 copy-done.1
  5.0 0.0 copy-start.2
  5.0 0.7 copy-done.2
  5.7 124.5 %shard_map.64 = bf16[2,1,16,1792]{3,2,1,0:T(8,128)(2,1)S(1)} custom-call(bf16[2,1,16,1792]{3,2,1,0:T(8,128)(2,1)S(1)} %copy-done.1, s32[2,1,16,8]{3,2,1,0:T(8,128)S(1)} %copy.7.ids, f32[1,1792]{1,0:T(1,128)S(1)} %copy-done.2, f32[1,1792,64]{2,1,0:T(8,128)S(1)} %copy.8.router, bf16[1792,1024]{1,0:T(8,128)(2,1)S(1)} %bitcast.2, bf16[1024,1792]{1,0:T(8,128)(2,1)} %bitcast.3), custom_call_target="tpu_custom_call" | custom-call | tf_op jit(solution)/shard_map/pallas_call | solution.py:290
  130.3 0.6 copy.10
Async XLA Ops:
  2.1 2.0 %copy-start = (bf16[1,1792,1024]{2,1,0:T(8,128)(2,1)S(1)}, bf16[1,1792,1024]{2,1,0:T(8,128)(2,1)}, u32[]{:S(2)}) copy-start(bf16[1,1792,1024]{2,1,0:T(8,128)(2,1)} %param.10) | copy-start | bytes 11010052
  4.1 0.9 copy-start.1
  5.0 0.7 copy-start.2

commit v2 on v1

v2 whole, which is shorter than its diff:
```python
import functools

import jax
import jax.numpy as jnp
from jax import lax
from jax.experimental import pallas as pl
from jax.experimental.pallas import tpu as pltpu
from jax.sharding import PartitionSpec as P

norm_eps = 1e-06
route_scale = 2.5
MESH = pl.DeviceIdType.MESH
BF = jnp.bfloat16
F32 = jnp.float32
LANES = 128


def over(v, n, limit):
    m = -(-65536 // n)
    assert all((i * m) >> 16 == i // n for i in range(limit))
    return (v * m) >> 16


def split3(v):
    hi = v.astype(BF)
    rest = v - hi.astype(F32)
    mid = rest.astype(BF)
    low = (rest - mid.astype(F32)).astype(BF)
    return hi, mid, low


def nt_dot(a, b):
    return lax.dot_general(a, b, (((1,), (1,)), ((), ())), preferred_element_type=F32)


def ahead(n):
    return sorted(range(1, n), key=lambda k: -min(k, n - k))


def groups(n):
    near = [k for k in range(n) if min(k, n - k) <= n // 4]
    return [near, [k for k in range(n) if k not in near]]


def mm(a, b):
    return jnp.dot(a, b, preferred_element_type=F32)


def layer(
    cfg, stream_h, ids_h, gain_h, router_h, w_up, w_down, out,
    stream, ids, gain, router, up, down, rparts, arr, blocks, codes, info, stat_s, stat_r, sel_s, rows, far_part, own_part,
    over_s, over_r, pair_s, pair_r, cross_r, act, made_s, made_r, mix_s, mix_r,
    w_sem, shift_ss, shift_rs, code_ss, code_rs, block_ss, block_rs, info_ss, info_rs, stat_ss, stat_rs,
    sel_ss, sel_rs, over_ss, over_rs, pair_ss, pair_rs, cross_rs, act_ss, act_rs, made_ss, made_rs, mix_ss, mix_rs,
):
    np_, nz, nx, nt, tok, cap, experts, width = cfg
    quarter = stream.shape[-1]
    ff = w_up.shape[-1]
    fq = ff // nt
    p = lax.axis_index("pipe")
    e = lax.axis_index("expert")
    t = lax.axis_index("tensor")
    z, x = e // nx, e % nx
    n1, n2 = (nx, nz), (nz, nx)
    c1, c2 = (x, z), (z, x)

    parts = groups(nx)
    sizes = [2 * len(ks) for ks in parts]
    firsts = [0, sizes[0]]
    per = nx * cap
    place = {}
    for g in range(2):
        for d in range(2):
            for i, k in enumerate(parts[g]):
                place[d, k] = firsts[g] + d * len(parts[g]) + i
    spans = [pl.ds(firsts[g] * per, sizes[g] * per) for g in range(2)]

    def at1(d, j):
        return z * nx + j if d == 0 else j * nx + x

    def at2(d, j):
        return j * nx + x if d == 0 else z * nx + j

    def to_expert(j):
        return {"expert": j}

    started = []

    def copy(src, dst, ss, rs, dev):
        c = pltpu.make_async_remote_copy(
            src_ref=src, dst_ref=dst, send_sem=ss, recv_sem=rs, device_id=dev, device_id_type=MESH
        )
        return c

    def send(*a):
        c = copy(*a)
        c.start()
        started.append(c)

    barrier = pltpu.get_barrier_semaphore()
    peers = [{"pipe": lax.rem(p + 1, np_)}, {"pipe": lax.rem(p + np_ - 1, np_)}]
    peers += [to_expert(at1(0, lax.rem(x + k, nx))) for k in range(1, nx)]
    peers += [to_expert(at2(0, lax.rem(z + k, nz))) for k in range(1, nz)]
    peers += [{"tensor": lax.rem(t + k, nt)} for k in range(1, nt)]
    for dev in peers:
        pl.semaphore_signal(barrier, inc=1, device_id=dev, device_id_type=MESH)
    loads = [
        pltpu.make_async_copy(a, b, w_sem.at[i])
        for i, (a, b) in enumerate(
            [(ids_h, ids), (stream_h, stream), (gain_h, gain), (router_h, router), (w_up, up), (w_down, down)]
        )
    ]
    for c in loads:
        c.start()
    cu, cd = loads[4:]

    loads[0].wait()
    row = lax.broadcasted_iota(jnp.int32, (LANES, tok), 0)
    ti = lax.broadcasted_iota(jnp.int32, (tok, tok), 0)
    tj = lax.broadcasted_iota(jnp.int32, (tok, tok), 1)
    before = (ti > tj).astype(F32).astype(BF)
    same = (ti == tj).astype(F32).astype(BF)
    named = []
    for d in range(2):
        chosen = ids[d, 0]
        turned = jnp.zeros((LANES, tok), F32)
        for k in range(chosen.shape[0]):
            turned = turned + (chosen[k : k + 1] == row).astype(F32)
        turned = turned.astype(BF)
        hot = nt_dot(same, turned)
        earlier = nt_dot(before, turned)
        named.append(hot)
        codes[d, c1[d]] = (hot * (earlier + 1.0)).astype(BF)
    loads[1].wait()
    loads[2].wait()
    loads[3].wait()
    for i, part in enumerate(split3(router[0] * gain[...])):
        rparts[i * experts : (i + 1) * experts] = part

    pl.semaphore_wait(barrier, len(peers))

    for d in range(2):
        dev = {"pipe": lax.rem(p + (1 if d == 0 else np_ - 1), np_)}
        send(stream.at[d, 0], arr.at[d], shift_ss.at[d], shift_rs.at[d], dev)
    for d in range(2):
        for k in ahead(n1[d]):
            j = lax.rem(c1[d] + k, n1[d])
            here = codes.at[d, c1[d]]
            send(here, here, code_ss.at[d, k], code_rs.at[d, k], to_expert(at1(d, j)))
    for d in range(2):
        copy(stream.at[d, 0], arr.at[d], shift_ss.at[d], shift_rs.at[d], {"pipe": p}).wait_recv()
        for k in ahead(n1[d]):
            j = lax.rem(c1[d] + k, n1[d])
            send(arr.at[d], blocks.at[d, c1[d]], block_ss.at[d, k], block_rs.at[d, k], to_expert(at1(d, j)))
        blocks[d, c1[d]] = arr[d]

    raw = jnp.concatenate([arr[0], arr[1]], axis=0)
    both = raw.astype(F32)
    squares = jnp.sum(both * both, axis=-1, keepdims=True)
    n = 2 * tok
    prod = nt_dot(raw, rparts[...])
    partial = prod[:, :experts] + (prod[:, experts : 2 * experts] + prod[:, 2 * experts : 3 * experts])
    stat_s[:, :experts] = partial
    stat_s[:, experts:] = jnp.broadcast_to(squares, (n, LANES - experts))
    for k in range(1, nt):
        send(stat_s, stat_r.at[k], stat_ss.at[k], stat_rs.at[k], {"tensor": lax.rem(t + k, nt)})
    total = stat_s[...]
    for k in range(1, nt):
        copy(stat_s, stat_r.at[k], stat_ss.at[k], stat_rs.at[k], {"tensor": t}).wait_recv()
        total = total + stat_r[k]
    inverse = lax.rsqrt(total[:, experts : experts + 1] / width + norm_eps)
    hot = jnp.concatenate(named, axis=0)
    scores = jax.nn.sigmoid(total * inverse) * hot
    gates = route_scale * scores / jnp.sum(scores, axis=-1, keepdims=True)
    lane2 = lax.broadcasted_iota(jnp.int32, (n, LANES), 1)
    both_info = jnp.where(lane2 < experts, gates, jnp.broadcast_to(inverse, (n, LANES)))
    for d in range(2):
        info[d, c1[d]] = both_info[d * tok : (d + 1) * tok]
        for k in ahead(n1[d]):
            j = lax.rem(c1[d] + k, n1[d])
            here = info.at[d, c1[d]]
            send(here, here, info_ss.at[d, k], info_rs.at[d, k], to_expert(at1(d, j)))

    weights = []
    for d in range(2):
        a, b = n1[d], n2[d]
        nr, nc = a * b * cap, a * tok
        for k in range(1, a):
            j = lax.rem(c1[d] + a - k, a)
            copy(codes.at[d, j], codes.at[d, j], code_ss.at[d, k], code_rs.at[d, k], to_expert(e)).wait_recv()
        code = codes[d].reshape(nc, LANES)
        rr = lax.broadcasted_iota(jnp.int32, (nr, LANES), 0)
        at = at2(d, over(rr, per, nr))
        pick = (lax.broadcasted_iota(jnp.int32, (nr, LANES), 1) == at).astype(F32).astype(BF)

        def chosen_of(shape, rdim, value):
            r = lax.broadcasted_iota(jnp.int32, shape, rdim)
            c = lax.broadcasted_iota(jnp.int32, shape, 1 - rdim)
            third = over(r, cap, nr)
            slot = r - third * cap
            block = third - over(r, per, nr) * a
            return (value == (slot + 1).astype(F32)) & (block == over(c, tok, nc))

        sel = chosen_of((nr, nc), 0, nt_dot(pick, code)).astype(F32).astype(BF)
        keep = chosen_of((nc, nr), 1, nt_dot(code, pick))
        for k in range(1, a):
            j = lax.rem(c1[d] + a - k, a)
            copy(info.at[d, j], info.at[d, j], info_ss.at[d, k], info_rs.at[d, k], to_expert(e)).wait_recv()
        facts = info[d].reshape(nc, LANES)
        ghi = facts.astype(BF)
        glo = (facts - ghi.astype(F32)).astype(BF)
        whi = jnp.where(keep, nt_dot(ghi, pick), 0.0).astype(BF)
        wlo = jnp.where(keep, nt_dot(glo, pick), 0.0).astype(BF)
        weights.append((whi, wlo))
        for k in range(1, a):
            j = lax.rem(c1[d] + a - k, a)
            copy(arr.at[d], blocks.at[d, j], block_ss.at[d, k], block_rs.at[d, k], to_expert(e)).wait_recv()
        inv = facts[:, experts : experts + 1]
        hidden = (blocks[d].reshape(nc, quarter).astype(F32) * gain[...] * inv).astype(BF)
        picked = mm(sel, hidden)
        for j in range(b):
            sel_s[d, j] = picked[j * per : (j + 1) * per].astype(BF)
    for g in range(2):
        for k in ahead(n2[0]):
            if k in parts[g]:
                for d in range(2):
                    j = lax.rem(c2[d] + k, n2[d])
                    send(sel_s.at[d, j], rows.at[place[d, k]], sel_ss.at[d, k], sel_rs.at[d, k], to_expert(at2(d, j)))
    for d in range(2):
        rows[place[d, 0]] = sel_s[d, c2[d]]

    end = (t == 0) | (t == nt - 1)
    pair = t + 1 - 2 * (t % 2)
    flip, turn = nt - 1 - t, lax.rem(t + 2, nt)
    far_end = jnp.where(end, flip, turn)
    far_mid = jnp.where(end, turn, flip)

    def columns(q):
        return up[:, pl.ds(pl.multiple_of(q * fq, fq), fq)]

    def over_copy(g):
        o = over_s.at[:, spans[g]]
        return copy(o, over_r.at[:, spans[g]], over_ss.at[g, 0], over_rs.at[g], {"tensor": pair})

    def pair_copy(g):
        return copy(pair_s.at[spans[g]], pair_r.at[spans[g]], pair_ss.at[g], pair_rs.at[g], {"tensor": pair})

    def cross_copy(g, i, q):
        return copy(over_s.at[i, spans[g]], cross_r.at[spans[g]], over_ss.at[g, i], cross_rs.at[g], {"tensor": q})

    def act_copy(g, q, i, o, to):
        c = act.at[q, spans[g]]
        return copy(c, c, act_ss.at[g, o], act_rs.at[g, i], {"tensor": to})

    def go(c):
        c.start()
        started.append(c)

    def arrive(g):
        for d in range(2):
            for k in parts[g]:
                if k:
                    copy(sel_s.at[d, 0], rows.at[place[d, k]], sel_ss.at[d, k], sel_rs.at[d, k], to_expert(e)).wait_recv()

    def upward(g):
        count = sizes[g]
        lhs = rows[firsts[g] : firsts[g] + count].reshape(count * per, quarter)
        for i, q in enumerate((far_end, far_mid)):
            far_part[i, spans[g]] = mm(lhs, columns(q))

        @pl.when(end)
        def _():
            over_s[:, spans[g]] = far_part[:, spans[g]].astype(BF)
            over_copy(g).start()

        pair_s[spans[g]] = mm(lhs, columns(pair)).astype(BF)
        go(pair_copy(g))
        own_part[spans[g]] = mm(lhs, columns(t))

    def combine(g):
        @pl.when(jnp.logical_not(end))
        def _():
            over_copy(g).wait_recv()
            over_s[:, spans[g]] = (far_part[:, spans[g]] + over_r[:, spans[g]].astype(F32)).astype(BF)
            cross_copy(g, 0, far_end).start()
            cross_copy(g, 1, far_mid).start()

    def activate(g):
        pair_copy(g).wait_recv()
        cross_copy(g, 0, t).wait_recv()
        inner = own_part[spans[g]] + pair_r[spans[g]].astype(F32) + cross_r[spans[g]].astype(F32)
        act[t, spans[g]] = jax.nn.silu(inner).astype(BF)

        @pl.when(end)
        def _():
            act_copy(g, t, 2, 1, far_mid).start()

        @pl.when(jnp.logical_not(end))
        def _():
            act_copy(g, t, 1, 1, far_mid).start()

        go(act_copy(g, t, 0, 0, pair))

    def relay(g):
        @pl.when(jnp.logical_not(end))
        def _():
            act_copy(g, far_mid, 1, 2, t).wait_recv()
            act_copy(g, far_mid, 1, 2, pair).start()
            act_copy(g, far_end, 2, 3, t).wait_recv()
            act_copy(g, far_end, 2, 3, pair).start()

    def downward(g):
        act_copy(g, pair, 0, 0, t).wait_recv()

        @pl.when(end)
        def _():
            act_copy(g, far_mid, 1, 2, t).wait_recv()
            act_copy(g, far_end, 2, 3, t).wait_recv()

        lhs = jnp.concatenate([act[q, spans[g]] for q in range(nt)], axis=1)
        step = min(256, quarter)
        for s in range(0, quarter, step):
            made = mm(lhs, down[:, s : s + step])
            for j in range(sizes[g]):
                made_s[firsts[g] + j, :, s : s + step] = made[j * per : (j + 1) * per].astype(BF)
        for k in sorted(parts[g], key=lambda k: -min(k, n2[0] - k)):
            for d in range(2):
                here = made_s.at[place[d, k]]
                if k:
                    j = lax.rem(c2[d] + n2[d] - k, n2[d])
                    send(here, made_r.at[d, c2[d]], made_ss.at[d, k], made_rs.at[d, k], to_expert(at2(d, j)))
                else:
                    made_r[d, c2[d]] = made_s[place[d, k]]

    cu.wait()
    cd.wait()
    arrive(0)
    upward(0)
    combine(0)
    arrive(1)
    upward(1)
    activate(0)
    combine(1)
    relay(0)
    activate(1)
    downward(0)
    relay(1)
    downward(1)
    for g in range(2):
        act_copy(g, t, 1, 1, far_mid).wait_send()

        @pl.when(end)
        def _():
            over_copy(g).wait_send()

        @pl.when(jnp.logical_not(end))
        def _():
            cross_copy(g, 0, far_end).wait_send()
            cross_copy(g, 1, far_mid).wait_send()
            act_copy(g, far_mid, 1, 2, pair).wait_send()
            act_copy(g, far_end, 2, 3, pair).wait_send()

    for d in range(2):
        a, b = n1[d], n2[d]
        nr = a * b * cap
        for k in range(1, b):
            j = lax.rem(c2[d] + k, b)
            copy(made_s.at[0], made_r.at[d, j], made_ss.at[d, k], made_rs.at[d, k], to_expert(e)).wait_recv()
        back = made_r[d].reshape(nr, quarter)
        whi, wlo = weights[d]
        mixed = mm(whi, back) + mm(wlo, back)
        for j in range(a):
            mix_s[d, j] = mixed[j * tok : (j + 1) * tok].astype(BF)
        for k in ahead(a):
            j = lax.rem(c1[d] + k, a)
            send(mix_s.at[d, j], mix_r.at[d, k], mix_ss.at[d, k], mix_rs.at[d, k], to_expert(at1(d, j)))
    for d in range(2):
        total = mix_s[d, c1[d]].astype(F32)
        for k in range(1, n1[d]):
            copy(mix_s.at[d, 0], mix_r.at[d, k], mix_ss.at[d, k], mix_rs.at[d, k], to_expert(e)).wait_recv()
            total = total + mix_r[d, k].astype(F32)
        out[d, 0] = (arr[d].astype(F32) + total).astype(BF)
    for c in started:
        c.wait_send()


def solution(mesh, nz=8, nx=8, cap=3):
    np_, nt = mesh.shape["pipe"], mesh.shape["tensor"]

    def shards(stream, ids, gain, router, w_up, w_down):
        tok, quarter = stream.shape[2:]
        experts, ff = router.shape[2], w_up.shape[2]
        cfg = (np_, nz, nx, nt, tok, cap, experts, float(quarter * nt))
        big, per = max(nz, nx), (nx * cap, nz * cap)
        assert nx == nz
        nr, fq = nx * nz * cap, ff // nt
        V, S = pltpu.VMEM, pltpu.SemaphoreType.DMA
        whole = pl.BlockSpec(memory_space=V)
        far = pl.BlockSpec(memory_space=pl.ANY)
        vmem = [
            V(stream.shape, BF), V((2, 1, ids.shape[3], tok), jnp.int32), V(gain.shape, F32), V((1, experts, quarter), F32),
            V((quarter, ff), BF), V((ff, quarter), BF), V((3 * experts, quarter), BF),
            V((2, tok, quarter), BF), V((2, big, tok, quarter), BF), V((2, big, tok, LANES), BF), V((2, big, tok, LANES), F32),
            V((2 * tok, LANES), F32), V((nt, 2 * tok, LANES), F32),
            V((2, big, per[0], quarter), BF), V((2 * big, per[0], quarter), BF),
            V((2, 2 * nr, fq), F32), V((2 * nr, fq), F32),
            V((2, 2 * nr, fq), BF), V((2, 2 * nr, fq), BF), V((2 * nr, fq), BF), V((2 * nr, fq), BF), V((2 * nr, fq), BF),
            V((nt, 2 * nr, fq), BF),
            V((2 * big, per[0], quarter), BF), V((2, big, per[0], quarter), BF),
            V((2, big, tok, quarter), BF), V((2, big, tok, quarter), BF),
        ]
        sems = [S((6,)), S((2,)), S((2,))] + [S((2, big))] * 6 + [S((nt,))] * 2 + [S((2, big))] * 2 + [S((2, 2))] + [S((2,))] * 4 + [S((2, 4))] * 2 + [S((2, big))] * 4
        return pl.pallas_call(
            functools.partial(layer, cfg),
            out_shape=jax.ShapeDtypeStruct(stream.shape, BF),
            in_specs=[far] * 6,
            out_specs=whole,
            scratch_shapes=vmem + sems,
            compiler_params=pltpu.CompilerParams(
                collective_id=0, has_side_effects=True, vmem_limit_bytes=67043328
            ),
        )(stream, jnp.swapaxes(ids, 2, 3), gain, jnp.swapaxes(router, 1, 2), w_up[0], w_down[0])

    return jax.shard_map(
        shards,
        mesh=mesh,
        in_specs=(
            P(None, "pipe", "expert", "tensor"),
            P(None, "pipe", "expert", None),
            P("pipe", "tensor"),
            P("pipe", "tensor", None),
            P("expert", "tensor", None),
            P("expert", None, "tensor"),
        ),
        out_specs=P(None, "pipe", "expert", "tensor"),
        check_vma=False,
    )
```

time: 133 us -> 115 us (0.86)
  Pallas kernels: 125 us -> 111 us
  local copies, waits for them, and re-layouts: 6.36 us -> 1.55 us
    pallas_call x1, Pallas kernels: 125 us -> 111 us  [shards(): pl.pallas_call(functools.partial(layer, cfg), out_shape=jax.ShapeDtypeStr...]
    unnamed x9 -> x1, local copies, waits for them, and re-layouts: 6.36 us -> 1.55 us
where the time goes in v2:
time: 115 us; the launch traced here: 113 us
  Pallas kernels  111 us (97%)
  local copies, waits for them, and re-layouts  1.55 us (1%)
    pallas_call x1, Pallas kernels, shards(): pl.pallas_call(functools.partial(layer, cfg), out_shape=jax.ShapeDtypeStr...  111 us

profile of v2, /device:TPU:1, one launch (start us, length us, event | category | flops | bytes accessed | tf_op | source)
XLA Modules:
  0.0 112.9 jit_solution(11394621759698166644)
XLA Ops:
  0.0 111.3 %shard_map.64 = bf16[2,1,16,1792]{3,2,1,0:T(8,128)(2,1)} custom-call(bf16[2,1,16,1792]{3,2,1,0:T(8,128)(2,1)} %stream_h.1, s32[2,1,8,16]{3,2,1,0:T(8,128)} %bitcast.7, f32[1,1792]{1,0:T(1,128)} %gain_h.1, f32[1,64,1792]{2,1,0:T(8,128)} %bitcast.6, bf16[1792,1024]{1,0:T(8,128)(2,1)} %bitcast.4, bf16[1024,1792]{1,0:T(8,128)(2,1)} %bitcast.5), custom_call_target="tpu_custom_call" | custom-call | tf_op jit(solution)/shard_map/pallas_call | solution.py:413
  111.3 1.6 %copy.8 = bf16[2,1,16,1792]{3,2,1,0:T(8,128)(2,1)} copy(bf16[2,1,16,1792]{3,2,1,0:T(8,128)(2,1)} %shard_map.64) | data formatting | bytes 229376

commit v3 on v2

v3 whole, which is shorter than its diff:
```python
import functools

import jax
import jax.numpy as jnp
from jax import lax
from jax.experimental import pallas as pl
from jax.experimental.pallas import tpu as pltpu
from jax.sharding import PartitionSpec as P

norm_eps = 1e-06
route_scale = 2.5
tree = (True, True, True)
passed = (True, True, False)
MESH = pl.DeviceIdType.MESH
BF = jnp.bfloat16
F32 = jnp.float32
LANES = 128


def over(v, n, limit):
    m = -(-65536 // n)
    assert all((i * m) >> 16 == i // n for i in range(limit))
    return (v * m) >> 16


def split3(v):
    hi = v.astype(BF)
    rest = v - hi.astype(F32)
    mid = rest.astype(BF)
    low = (rest - mid.astype(F32)).astype(BF)
    return hi, mid, low


def nt_dot(a, b):
    return lax.dot_general(a, b, (((1,), (1,)), ((), ())), preferred_element_type=F32)


def ahead(n):
    return sorted(range(1, n), key=lambda k: -min(k, n - k))


def groups(n):
    edge = n // 8
    away = [min(k, n - k) for k in range(n)]
    return [
        [k for k in range(n) if away[k] > edge + 1],
        [k for k in range(n) if away[k] <= edge],
        [k for k in range(n) if away[k] == edge + 1],
    ]


def mm(a, b):
    return jnp.dot(a, b, preferred_element_type=F32)


def layer(
    cfg, stream_h, ids_h, gain_h, router_h, w_up, w_down, out,
    stream, ids, gain, router, up, down, rparts, arr, blocks, codes, info, stat_s, stat_r, hots, mixers, sel_s, rows, far_part, own_part,
    over_s, over_r, pair_s, pair_r, cross_r, act, made_s, made_r, mix_s, mix_r,
    w_sem, shift_ss, shift_rs, code_ss, code_rs, block_ss, block_rs, info_ss, info_rs, stat_ss, stat_rs,
    sel_ss, sel_rs, over_ss, over_rs, pair_ss, pair_rs, cross_rs, act_ss, act_rs, made_ss, made_rs, mix_ss, mix_rs,
):
    np_, nz, nx, nt, tok, cap, experts, width = cfg
    quarter = stream.shape[-1]
    ff = w_up.shape[-1]
    fq = ff // nt
    p = lax.axis_index("pipe")
    e = lax.axis_index("expert")
    t = lax.axis_index("tensor")
    z, x = e // nx, e % nx
    n1, n2 = (nx, nz), (nz, nx)
    c1, c2 = (x, z), (z, x)

    def coord1(d):
        return x + d * (z - x)

    def coord2(d):
        return z + d * (x - z)

    parts = groups(nx)
    sizes = [2 * len(ks) for ks in parts]
    firsts = [sum(sizes[:g]) for g in range(3)]
    per = nx * cap
    place = {}
    for g in range(3):
        for d in range(2):
            for i, k in enumerate(parts[g]):
                place[d, k] = firsts[g] + d * len(parts[g]) + i
    spans = [pl.ds(firsts[g] * per, sizes[g] * per) for g in range(3)]

    def at1(d, j):
        return z * nx + j + d * (j * nx + x - z * nx - j)

    def at2(d, j):
        return j * nx + x + d * (z * nx + j - j * nx - x)

    def to_expert(j):
        return {"expert": j}

    started = []

    def copy(src, dst, ss, rs, dev):
        c = pltpu.make_async_remote_copy(
            src_ref=src, dst_ref=dst, send_sem=ss, recv_sem=rs, device_id=dev, device_id_type=MESH
        )
        return c

    def send(*a):
        c = copy(*a)
        c.start()
        started.append(c)

    barrier = pltpu.get_barrier_semaphore()
    peers = [{"pipe": lax.rem(p + 1, np_)}, {"pipe": lax.rem(p + np_ - 1, np_)}]
    peers += [to_expert(at1(0, lax.rem(x + k, nx))) for k in range(1, nx)]
    peers += [to_expert(at2(0, lax.rem(z + k, nz))) for k in range(1, nz)]
    peers += [{"tensor": lax.rem(t + k, nt)} for k in range(1, nt)]
    for dev in peers:
        pl.semaphore_signal(barrier, inc=1, device_id=dev, device_id_type=MESH)
    loads = [
        pltpu.make_async_copy(a, b, w_sem.at[i])
        for i, (a, b) in enumerate(
            [(ids_h, ids), (stream_h, stream), (gain_h, gain), (router_h, router), (w_up, up), (w_down, down)]
        )
    ]
    for c in loads:
        c.start()
    cu, cd = loads[4:]

    loads[0].wait()
    lane = lax.broadcasted_iota(jnp.int32, (tok, LANES), 1)
    row = lax.broadcasted_iota(jnp.int32, (LANES, tok), 0)
    ti = lax.broadcasted_iota(jnp.int32, (tok, tok), 0)
    tj = lax.broadcasted_iota(jnp.int32, (tok, tok), 1)
    before = (ti > tj).astype(F32).astype(BF)
    same = (ti == tj).astype(F32).astype(BF)
    for d in range(2):
        chosen = ids[d, 0]
        turned = jnp.zeros((LANES, tok), F32)
        for k in range(chosen.shape[0]):
            turned = turned + (chosen[k : k + 1] == row).astype(F32)
        turned = turned.astype(BF)
        hot = nt_dot(same, turned)
        earlier = nt_dot(before, turned)
        hots[d] = hot
        codes[d, c1[d]] = (hot * (earlier + 1.0)).astype(BF)
    loads[1].wait()
    pl.semaphore_wait(barrier, len(peers))

    for d in range(2):
        dev = {"pipe": lax.rem(p + (1 if d == 0 else np_ - 1), np_)}
        send(stream.at[d, 0], arr.at[d], shift_ss.at[d], shift_rs.at[d], dev)
    for d in range(2):
        for k in ahead(n1[d]):
            j = lax.rem(c1[d] + k, n1[d])
            here = codes.at[d, c1[d]]
            send(here, here, code_ss.at[d, k], code_rs.at[d, k], to_expert(at1(d, j)))
    loads[2].wait()
    loads[3].wait()
    for i, part in enumerate(split3(router[0] * gain[...])):
        rparts[i * experts : (i + 1) * experts] = part

    a = nx
    first = 1 - p % 2
    for d in (first, 1 - first):
        copy(stream.at[d, 0], arr.at[d], shift_ss.at[d], shift_rs.at[d], {"pipe": p}).wait_recv()
        own = coord1(d)
        for k in ahead(a):
            j = lax.rem(own + k, a)
            send(arr.at[d], blocks.at[d, own], block_ss.at[d, k], block_rs.at[d, k], to_expert(at1(d, j)))
        raw = arr[d]
        blocks[d, own] = raw
        wide = raw.astype(F32)
        squares = jnp.sum(wide * wide, axis=-1, keepdims=True)
        prod = nt_dot(raw, rparts[...])
        partial = prod[:, :experts] + (prod[:, experts : 2 * experts] + prod[:, 2 * experts : 3 * experts])
        stat_s[d, :, :experts] = partial
        stat_s[d, :, experts:] = jnp.broadcast_to(squares, (tok, LANES - experts))
        for k in range(1, nt):
            q = lax.rem(t + k, nt)
            send(stat_s.at[d], stat_r.at[d, k], stat_ss.at[d, k], stat_rs.at[d, k], {"tensor": q})
    for d in (first, 1 - first):
        total = stat_s[d]
        for k in range(1, nt):
            copy(stat_s.at[d], stat_r.at[d, k], stat_ss.at[d, k], stat_rs.at[d, k], {"tensor": t}).wait_recv()
            total = total + stat_r[d, k]
        inverse = lax.rsqrt(total[:, experts : experts + 1] / width + norm_eps)
        scores = jax.nn.sigmoid(total * inverse) * hots[d]
        gates = route_scale * scores / jnp.sum(scores, axis=-1, keepdims=True)
        own = coord1(d)
        info[d, own] = jnp.where(lane < experts, gates, jnp.broadcast_to(inverse, (tok, LANES)))
        for k in ahead(a):
            j = lax.rem(own + k, a)
            here = info.at[d, own]
            send(here, here, info_ss.at[d, k], info_rs.at[d, k], to_expert(at1(d, j)))

    b = nx
    nr, nc = a * b * cap, a * tok
    for d in (first, 1 - first):
        own = coord1(d)
        for k in range(1, a):
            j = lax.rem(own + a - k, a)
            copy(codes.at[d, j], codes.at[d, j], code_ss.at[d, k], code_rs.at[d, k], to_expert(e)).wait_recv()
        code = codes[d].reshape(nc, LANES)
        rr = lax.broadcasted_iota(jnp.int32, (nr, LANES), 0)
        at = at2(d, over(rr, per, nr))
        pick = (lax.broadcasted_iota(jnp.int32, (nr, LANES), 1) == at).astype(F32).astype(BF)

        def chosen_of(shape, rdim, value):
            r = lax.broadcasted_iota(jnp.int32, shape, rdim)
            c = lax.broadcasted_iota(jnp.int32, shape, 1 - rdim)
            third = over(r, cap, nr)
            slot = r - third * cap
            block = third - over(r, per, nr) * a
            return (value == (slot + 1).astype(F32)) & (block == over(c, tok, nc))

        sel = chosen_of((nr, nc), 0, nt_dot(pick, code)).astype(F32).astype(BF)
        keep = chosen_of((nc, nr), 1, nt_dot(code, pick))
        for k in range(1, a):
            j = lax.rem(own + a - k, a)
            copy(info.at[d, j], info.at[d, j], info_ss.at[d, k], info_rs.at[d, k], to_expert(e)).wait_recv()
        for k in range(1, a):
            j = lax.rem(own + a - k, a)
            copy(arr.at[d], blocks.at[d, j], block_ss.at[d, k], block_rs.at[d, k], to_expert(e)).wait_recv()
        facts = info[d].reshape(nc, LANES)
        inv = facts[:, experts : experts + 1]
        hidden = (blocks[d].reshape(nc, quarter).astype(F32) * gain[...] * inv).astype(BF)
        picked = mm(sel, hidden)
        for j in range(b):
            sel_s[d, j] = picked[j * per : (j + 1) * per].astype(BF)
        over2 = coord2(d)
        for g in range(3):
            for k in ahead(b):
                if k in parts[g]:
                    j = lax.rem(over2 + k, b)
                    to = rows.at[place[0, k] + d * len(parts[g])]
                    send(sel_s.at[d, j], to, sel_ss.at[d, k], sel_rs.at[d, k], to_expert(at2(d, j)))
        rows[place[0, 0] + d * len(parts[0])] = sel_s[d, over2]
        ghi = facts.astype(BF)
        glo = (facts - ghi.astype(F32)).astype(BF)
        mixers[d, 0] = jnp.where(keep, nt_dot(ghi, pick), 0.0).astype(BF)
        mixers[d, 1] = jnp.where(keep, nt_dot(glo, pick), 0.0).astype(BF)

    end = (t == 0) | (t == nt - 1)
    pair = t + 1 - 2 * (t % 2)
    flip, turn = nt - 1 - t, lax.rem(t + 2, nt)
    far_end = jnp.where(end, flip, turn)
    far_mid = jnp.where(end, turn, flip)

    def columns(q):
        return up[:, pl.ds(pl.multiple_of(q * fq, fq), fq)]

    side = (far_end, far_mid)

    def over_copy(g, i, q):
        o = over_s.at[i, spans[g]]
        return copy(o, over_r.at[i, spans[g]], over_ss.at[g, i], over_rs.at[g, i], {"tensor": q})

    def straight_copy(g, i, o, q):
        c = over_s.at[i, spans[g]]
        return copy(c, over_r.at[o, spans[g]], over_ss.at[g, i], over_rs.at[g, o], {"tensor": q})

    def pair_copy(g):
        return copy(pair_s.at[spans[g]], pair_r.at[spans[g]], pair_ss.at[g], pair_rs.at[g], {"tensor": pair})

    def cross_copy(g, i, q):
        return copy(over_s.at[i, spans[g]], cross_r.at[spans[g]], over_ss.at[g, i], cross_rs.at[g], {"tensor": q})

    def act_copy(g, q, i, o, to):
        c = act.at[q, spans[g]]
        return copy(c, c, act_ss.at[g, o], act_rs.at[g, i], {"tensor": to})

    def go(c):
        c.start()
        started.append(c)

    def at_end(f):
        pl.when(end)(f)

    def at_mid(f):
        pl.when(jnp.logical_not(end))(f)

    def arrive(g):
        for d in range(2):
            for k in parts[g]:
                if k:
                    copy(sel_s.at[d, 0], rows.at[place[d, k]], sel_ss.at[d, k], sel_rs.at[d, k], to_expert(e)).wait_recv()

    def upward(g):
        count = sizes[g]
        lhs = rows[firsts[g] : firsts[g] + count].reshape(count * per, quarter)
        for i in range(2):
            part = mm(lhs, columns(side[i]))
            if tree[g]:
                far_part[i, spans[g]] = part

                @at_end
                def _():
                    over_s[i, spans[g]] = far_part[i, spans[g]].astype(BF)
                    over_copy(g, i, pair).start()
            else:
                over_s[i, spans[g]] = part.astype(BF)
                at_end(lambda: straight_copy(g, i, 0, side[i]).start())
                at_mid(lambda: straight_copy(g, i, 1, side[i]).start())
        pair_s[spans[g]] = mm(lhs, columns(pair)).astype(BF)
        go(pair_copy(g))
        own_part[spans[g]] = mm(lhs, columns(t))

    def combine(g):
        if tree[g]:

            @at_mid
            def _():
                for i in range(2):
                    over_copy(g, i, t).wait_recv()
                    over_s[i, spans[g]] = (far_part[i, spans[g]] + over_r[i, spans[g]].astype(F32)).astype(BF)
                    cross_copy(g, i, side[i]).start()

    def activate(g):
        pair_copy(g).wait_recv()
        inner = own_part[spans[g]] + pair_r[spans[g]].astype(F32)
        if tree[g]:
            cross_copy(g, 0, t).wait_recv()
            inner = inner + cross_r[spans[g]].astype(F32)
        else:
            for o in range(2):
                straight_copy(g, 0, o, t).wait_recv()
                inner = inner + over_r[o, spans[g]].astype(F32)
        act[t, spans[g]] = jax.nn.silu(inner).astype(BF)

        @at_end
        def _():
            if not passed[g]:
                act_copy(g, t, 2, 2, far_end).start()
            act_copy(g, t, 2, 1, far_mid).start()

        @at_mid
        def _():
            if not passed[g]:
                act_copy(g, t, 1, 2, far_end).start()
            act_copy(g, t, 1, 1, far_mid).start()

        go(act_copy(g, t, 0, 0, pair))

    def relay(g):
        if passed[g]:

            @at_mid
            def _():
                act_copy(g, far_mid, 1, 2, t).wait_recv()
                act_copy(g, far_mid, 1, 2, pair).start()
                act_copy(g, far_end, 2, 3, t).wait_recv()
                act_copy(g, far_end, 2, 3, pair).start()

    def downward(g):
        def rest():
            act_copy(g, far_mid, 1, 2, t).wait_recv()
            act_copy(g, far_end, 2, 3, t).wait_recv()

        act_copy(g, pair, 0, 0, t).wait_recv()
        if passed[g]:
            at_end(rest)
        else:
            rest()
        lhs = jnp.concatenate([act[q, spans[g]] for q in range(nt)], axis=1)
        step = min(256, quarter)
        for s in range(0, quarter, step):
            made = mm(lhs, down[:, s : s + step])
            for j in range(sizes[g]):
                made_s[firsts[g] + j, :, s : s + step] = made[j * per : (j + 1) * per].astype(BF)
        for k in sorted(parts[g], key=lambda k: -min(k, n2[0] - k)):
            for d in range(2):
                here = made_s.at[place[d, k]]
                if k:
                    j = lax.rem(c2[d] + n2[d] - k, n2[d])
                    send(here, made_r.at[d, c2[d]], made_ss.at[d, k], made_rs.at[d, k], to_expert(at2(d, j)))
                else:
                    made_r[d, c2[d]] = made_s[place[d, k]]

    cu.wait()
    arrive(0)
    upward(0)
    combine(0)
    arrive(1)
    upward(1)
    activate(0)
    combine(1)
    arrive(2)
    upward(2)
    relay(0)
    activate(1)
    combine(2)
    cd.wait()
    downward(0)
    relay(1)
    activate(2)
    downward(1)
    relay(2)
    downward(2)
    for g in range(3):
        act_copy(g, t, 1, 1, far_mid).wait_send()
        over_copy(g, 0, pair).wait_send()
        over_copy(g, 1, pair).wait_send()
        if passed[g]:

            @at_mid
            def _():
                act_copy(g, far_mid, 1, 2, pair).wait_send()
                act_copy(g, far_end, 2, 3, pair).wait_send()
        else:
            act_copy(g, t, 1, 2, far_end).wait_send()

    for d in range(2):
        a, b = n1[d], n2[d]
        nr = a * b * cap
        for k in range(1, b):
            j = lax.rem(c2[d] + k, b)
            copy(made_s.at[0], made_r.at[d, j], made_ss.at[d, k], made_rs.at[d, k], to_expert(e)).wait_recv()
        back = made_r[d].reshape(nr, quarter)
        mixed = mm(mixers[d, 0], back) + mm(mixers[d, 1], back)
        for j in range(a):
            mix_s[d, j] = mixed[j * tok : (j + 1) * tok].astype(BF)
        for k in ahead(a):
            j = lax.rem(c1[d] + k, a)
            send(mix_s.at[d, j], mix_r.at[d, k], mix_ss.at[d, k], mix_rs.at[d, k], to_expert(at1(d, j)))
    for d in range(2):
        total = mix_s[d, c1[d]].astype(F32)
        for k in range(1, n1[d]):
            copy(mix_s.at[d, 0], mix_r.at[d, k], mix_ss.at[d, k], mix_rs.at[d, k], to_expert(e)).wait_recv()
            total = total + mix_r[d, k].astype(F32)
        out[d, 0] = (arr[d].astype(F32) + total).astype(BF)
    for c in started:
        c.wait_send()


def solution(mesh, nz=8, nx=8, cap=3):
    np_, nt = mesh.shape["pipe"], mesh.shape["tensor"]

    def shards(stream, ids, gain, router, w_up, w_down):
        tok, quarter = stream.shape[2:]
        experts, ff = router.shape[2], w_up.shape[2]
        cfg = (np_, nz, nx, nt, tok, cap, experts, float(quarter * nt))
        big, per = max(nz, nx), (nx * cap, nz * cap)
        assert nx == nz
        nr, fq = nx * nz * cap, ff // nt
        V, S = pltpu.VMEM, pltpu.SemaphoreType.DMA
        whole = pl.BlockSpec(memory_space=V)
        far = pl.BlockSpec(memory_space=pl.ANY)
        vmem = [
            V(stream.shape, BF), V((2, 1, ids.shape[3], tok), jnp.int32), V(gain.shape, F32), V((1, experts, quarter), F32),
            V((quarter, ff), BF), V((ff, quarter), BF), V((3 * experts, quarter), BF),
            V((2, tok, quarter), BF), V((2, big, tok, quarter), BF), V((2, big, tok, LANES), BF), V((2, big, tok, LANES), F32),
            V((2, tok, LANES), F32), V((2, nt, tok, LANES), F32), V((2, tok, LANES), F32), V((2, 2, big * tok, nr), BF),
            V((2, big, per[0], quarter), BF), V((2 * big, per[0], quarter), BF),
            V((2, 2 * nr, fq), F32), V((2 * nr, fq), F32),
            V((2, 2 * nr, fq), BF), V((2, 2 * nr, fq), BF), V((2 * nr, fq), BF), V((2 * nr, fq), BF), V((2 * nr, fq), BF),
            V((nt, 2 * nr, fq), BF),
            V((2 * big, per[0], quarter), BF), V((2, big, per[0], quarter), BF),
            V((2, big, tok, quarter), BF), V((2, big, tok, quarter), BF),
        ]
        sems = [S((6,)), S((2,)), S((2,))] + [S((2, big))] * 6 + [S((2, nt))] * 2 + [S((2, big))] * 2 + [S((3, 2))] * 2 + [S((3,))] * 3 + [S((3, 4))] * 2 + [S((2, big))] * 4
        return pl.pallas_call(
            functools.partial(layer, cfg),
            out_shape=pltpu.VMEM(stream.shape, BF),
            in_specs=[pl.BlockSpec(memory_space=pltpu.HBM)] * 6,
            out_specs=whole,
            scratch_shapes=vmem + sems,
            compiler_params=pltpu.CompilerParams(
                collective_id=0, has_side_effects=True, vmem_limit_bytes=56 * 1024 * 1024
            ),
        )(stream, jnp.swapaxes(ids, 2, 3), gain, jnp.swapaxes(router, 1, 2), w_up[0], w_down[0])

    return jax.shard_map(
        shards,
        mesh=mesh,
        in_specs=(
            P(None, "pipe", "expert", "tensor"),
            P(None, "pipe", "expert", None),
            P("pipe", "tensor"),
            P("pipe", "tensor", None),
            P("expert", "tensor", None),
            P("expert", None, "tensor"),
        ),
        out_specs=P(None, "pipe", "expert", "tensor"),
        check_vma=False,
    )
```

time: 115 us -> 99.9 us (0.87); the launches traced: 113 us -> 99.8 us
  Pallas kernels: 111 us -> 99.1 us
    pallas_call x1, Pallas kernels: 111 us -> 99.1 us  [shards(): pl.pallas_call(functools.partial(layer, cfg), out_shape=pltpu.VMEM(stream...]
where the time goes in v3:
time: 99.9 us; the launch traced here: 99.8 us
  Pallas kernels  99.1 us (99%)
    pallas_call x1, Pallas kernels, shards(): pl.pallas_call(functools.partial(layer, cfg), out_shape=pltpu.VMEM(stream...  99.1 us

profile of v3, /device:TPU:1, one launch (start us, length us, event | category | flops | bytes accessed | tf_op | source)
XLA Modules:
  0.0 99.8 jit_solution(11300555565411238533)
XLA Ops:
  0.0 99.1 %shard_map.64 = bf16[2,1,16,1792]{3,2,1,0:T(8,128)(2,1)S(1)} custom-call(bf16[2,1,16,1792]{3,2,1,0:T(8,128)(2,1)} %stream_h.1, s32[2,1,8,16]{3,2,1,0:T(8,128)} %bitcast.7, f32[1,1792]{1,0:T(1,128)} %gain_h.1, f32[1,64,1792]{2,1,0:T(8,128)} %bitcast.6, bf16[1792,1024]{1,0:T(8,128)(2,1)} %bitcast.4, bf16[1024,1792]{1,0:T(8,128)(2,1)} %bitcast.5), custom_call_target="tpu_custom_call" | custom-call | tf_op jit(solution)/shard_map/pallas_call | solution.py:462
  99.1 0.6 copy.8

commit v4 on v3

--- a/solution.py
+++ b/solution.py
@@ -410,22 +410,21 @@
         else:
             act_copy(g, t, 1, 2, far_end).wait_send()
 
-    for d in range(2):
-        a, b = n1[d], n2[d]
-        nr = a * b * cap
+    for d in (first, 1 - first):
+        own, mine = coord1(d), coord2(d)
         for k in range(1, b):
-            j = lax.rem(c2[d] + k, b)
+            j = lax.rem(mine + k, b)
             copy(made_s.at[0], made_r.at[d, j], made_ss.at[d, k], made_rs.at[d, k], to_expert(e)).wait_recv()
         back = made_r[d].reshape(nr, quarter)
         mixed = mm(mixers[d, 0], back) + mm(mixers[d, 1], back)
         for j in range(a):
             mix_s[d, j] = mixed[j * tok : (j + 1) * tok].astype(BF)
         for k in ahead(a):
-            j = lax.rem(c1[d] + k, a)
+            j = lax.rem(own + k, a)
             send(mix_s.at[d, j], mix_r.at[d, k], mix_ss.at[d, k], mix_rs.at[d, k], to_expert(at1(d, j)))
-    for d in range(2):
-        total = mix_s[d, c1[d]].astype(F32)
-        for k in range(1, n1[d]):
+    for d in (first, 1 - first):
+        total = mix_s[d, coord1(d)].astype(F32)
+        for k in range(1, a):
             copy(mix_s.at[d, 0], mix_r.at[d, k], mix_ss.at[d, k], mix_rs.at[d, k], to_expert(e)).wait_recv()
             total = total + mix_r[d, k].astype(F32)
         out[d, 0] = (arr[d].astype(F32) + total).astype(BF)

time: 99.9 us -> 101 us (1.011)
  no operation moved by 1% of the time
where the time goes in v4:
time: 101 us
  Pallas kernels  100 us (99%)
    pallas_call x1, Pallas kernels, shards(): pl.pallas_call(functools.partial(layer, cfg), out_shape=pltpu.VMEM(stream...  100 us

profile of v4, /device:TPU:1, one launch (start us, length us, event | category | flops | bytes accessed | tf_op | source)
XLA Modules:
  0.0 100.8 jit_solution(1860305664219097261)
XLA Ops:
  0.0 100.1 %shard_map.64 = bf16[2,1,16,1792]{3,2,1,0:T(8,128)(2,1)S(1)} custom-call(bf16[2,1,16,1792]{3,2,1,0:T(8,128)(2,1)} %stream_h.1, s32[2,1,8,16]{3,2,1,0:T(8,128)} %bitcast.7, f32[1,1792]{1,0:T(1,128)} %gain_h.1, f32[1,64,1792]{2,1,0:T(8,128)} %bitcast.6, bf16[1792,1024]{1,0:T(8,128)(2,1)} %bitcast.4, bf16[1024,1792]{1,0:T(8,128)(2,1)} %bitcast.5), custom_call_target="tpu_custom_call" | custom-call | tf_op jit(solution)/shard_map/pallas_call | solution.py:461
  100.1 0.6 copy.8
